TPU v7x, 8 devices: a whole 2x2x1 slice. The times are simulated.
8 devices in a mesh: part: 1 (over z), row: 2 (over y), col: 2 (over x), core: 2 (over core).
Axes of the slice: x: 2, y: 2, z: 1, core: 2. Of those that a mesh axis runs over, the one named last changes fastest.
Arguments:
- tokens: bfloat16 [4096, 512], P(('part', 'row', 'col', 'core'))
- route_idx: int32 [4096, 8], P(('part', 'row', 'col', 'core'))
- gate_vals: float32 [4096, 8], P(('part', 'row', 'col', 'core'))
- w_gate: bfloat16 [64, 512, 384], P(('row', 'col', 'core'))
- w_up: bfloat16 [64, 512, 384], P(('row', 'col', 'core'))
- w_down: bfloat16 [64, 384, 512], P(('row', 'col', 'core'))
- grad_out: bfloat16 [4096, 512], P(('part', 'row', 'col', 'core'))
Outputs:
- output 1: bfloat16 [4096, 512], P(('part', 'row', 'col', 'core'))
- output 2: bfloat16 [4096, 512], P(('part', 'row', 'col', 'core'))
- output 3: float32 [4096, 8], P(('part', 'row', 'col', 'core'))
- output 4: float32 [64, 512, 384], P(('part', 'row', 'col', 'core'))
- output 5: float32 [64, 512, 384], P(('part', 'row', 'col', 'core'))
- output 6: float32 [64, 384, 512], P(('part', 'row', 'col', 'core'))
All inputs are finite; a program needn't handle non-finite values.
Results may differ from a plain program's by a relative error of at most 0.0119401.
Values are sent between devices in bfloat16 or wider.
A program may use at most 1 GiB of HBM per device.

v0:
```python
import jax
import jax.numpy as jnp
from jax import lax
from jax.sharding import PartitionSpec as P

EP_AXES = ('row', 'col', 'core')
ALL_AXES = ('part', 'row', 'col', 'core')
HOT_SLOTS = 2


def slot_capacity(dev_tokens, top_k, experts, ep_devs):
    hot_load = dev_tokens * ep_devs // experts
    cold_experts = experts - 2 * experts // ep_devs
    cold_load = -(-(dev_tokens * (top_k - HOT_SLOTS)) // cold_experts)
    return max(hot_load, cold_load)


def swiglu(gate_h, up_h):
    return (jax.nn.silu(gate_h.astype(jnp.float32)) * up_h.astype(jnp.float32)).astype(jnp.bfloat16)


def pack_slots(route_loc, ep_devs, local_experts, capacity):
    flat_ids = route_loc.reshape(-1)
    slot_count = flat_ids.shape[0]
    experts = ep_devs * local_experts
    onehot = (flat_ids[:, None] == jnp.arange(experts, dtype=jnp.int32)[None, :]).astype(jnp.int32)
    rank_in = jnp.sum((jnp.cumsum(onehot, axis=0) - onehot) * onehot, axis=1)
    slot_dest = ((flat_ids % local_experts) * ep_devs + flat_ids // local_experts) * capacity + rank_in
    buf_slots = jnp.full((experts * capacity,), slot_count, jnp.int32).at[slot_dest].set(jnp.arange(slot_count, dtype=jnp.int32))
    return slot_dest, buf_slots


def solution(mesh):
    ep_devs = mesh.shape['row'] * mesh.shape['col'] * mesh.shape['core']
    tok_spec = P(ALL_AXES, None)
    w_spec = P(EP_AXES, None, None)
    gw_spec = P(ALL_AXES, None, None)

    def exchange(send_buf):
        return lax.all_to_all(send_buf, EP_AXES, 1, 1, tiled=True)

    def local_step(tokens, route_idx, gate_vals, w_gate, w_up, w_down, grad_out):
        dev_tokens, top_k = route_idx.shape
        model_dim = tokens.shape[1]
        local_experts = w_gate.shape[0]
        experts = local_experts * ep_devs
        slot_count = dev_tokens * top_k
        capacity = slot_capacity(dev_tokens, top_k, experts, ep_devs)
        buf_shape = (local_experts, ep_devs, capacity, model_dim)
        flat_shape = (local_experts, ep_devs * capacity, model_dim)
        slot_dest, buf_slots = pack_slots(route_idx, ep_devs, local_experts, capacity)
        send_x = jnp.take(tokens, buf_slots // top_k, axis=0, mode='fill', fill_value=0).reshape(buf_shape)
        recv_x = exchange(send_x).reshape(flat_shape)
        gate_h = jnp.einsum('lmd,ldf->lmf', recv_x, w_gate, preferred_element_type=jnp.float32).astype(jnp.bfloat16)
        up_h = jnp.einsum('lmd,ldf->lmf', recv_x, w_up, preferred_element_type=jnp.float32).astype(jnp.bfloat16)
        hidden, act_vjp = jax.vjp(swiglu, gate_h, up_h)
        expert_out = jnp.einsum('lmf,lfd->lmd', hidden, w_down, preferred_element_type=jnp.float32).astype(jnp.bfloat16)
        back_out = exchange(expert_out.reshape(buf_shape))
        slot_out = jnp.take(back_out.reshape(-1, model_dim), slot_dest, axis=0).reshape(dev_tokens, top_k, model_dim)
        moe_out = jnp.einsum('tj,tjd->td', gate_vals, slot_out, preferred_element_type=jnp.float32).astype(jnp.bfloat16)
        grad_gates = jnp.einsum('td,tjd->tj', grad_out, slot_out, preferred_element_type=jnp.float32)
        slot_grad = (gate_vals[:, :, None] * grad_out[:, None, :].astype(jnp.float32)).astype(jnp.bfloat16).reshape(slot_count, model_dim)
        send_g = jnp.take(slot_grad, buf_slots, axis=0, mode='fill', fill_value=0).reshape(buf_shape)
        recv_g = exchange(send_g).reshape(flat_shape)
        d_hidden = jnp.einsum('lmd,lfd->lmf', recv_g, w_down, preferred_element_type=jnp.float32).astype(jnp.bfloat16)
        d_gate_h, d_up_h = act_vjp(d_hidden)
        grad_w_down = jnp.einsum('lmf,lmd->lfd', hidden, recv_g, preferred_element_type=jnp.float32)
        grad_w_gate = jnp.einsum('lmd,lmf->ldf', recv_x, d_gate_h, preferred_element_type=jnp.float32)
        grad_w_up = jnp.einsum('lmd,lmf->ldf', recv_x, d_up_h, preferred_element_type=jnp.float32)
        part_grad = (jnp.einsum('lmf,ldf->lmd', d_gate_h, w_gate, preferred_element_type=jnp.float32) + jnp.einsum('lmf,ldf->lmd', d_up_h, w_up, preferred_element_type=jnp.float32)).astype(jnp.bfloat16)
        back_g = exchange(part_grad.reshape(buf_shape))
        slot_dx = jnp.take(back_g.reshape(-1, model_dim), slot_dest, axis=0).reshape(dev_tokens, top_k, model_dim)
        grad_tokens = jnp.sum(slot_dx.astype(jnp.float32), axis=1).astype(jnp.bfloat16)
        return moe_out, grad_tokens, grad_gates, grad_w_gate, grad_w_up, grad_w_down

    return jax.shard_map(local_step, mesh=mesh, in_specs=(tok_spec, tok_spec, tok_spec, w_spec, w_spec, w_spec, tok_spec), out_specs=(tok_spec, tok_spec, tok_spec, gw_spec, gw_spec, gw_spec), check_vma=False)
```

profile of v0, /device:TPU:0, one launch (start us, length us, event | category | flops | bytes accessed | tf_op | source)
XLA Modules:
  0.0 347.9 jit_solution(5483603996642443195)
XLA Ops:
  3.2 35.3 %reduce-window.6 = s32[64,32,128]{2,1,0:T(8,128)} reduce-window(s32[64,32,128]{2,1,0:T(8,128)} %fusion.17, s32[]{:T(128)} %constant.79.clone.1), window={size=1x1x128 pad=0_0x0_0x127_0}, to_apply=%region_0.0 | reduce-window | flops 33292288 | bytes 2097156 | tf_op jit(solution)/shard_map/reduce-window
  45.5 15.5 %scatter_custom_fusion = s32[4096]{0:T(1024)S(1)} fusion(s32[4096]{0:T(1024)S(1)} %bitcast.82, s32[4096]{0:T(1024)S(1)} %iota.11, s32[]{:T(128)} %constant.78.clone.1), kind=kCustom, calls=%fused_computation.83 | custom fusion | bytes 16388 | tf_op jit(solution)/shard_map/scatter | solution.py:29
  61.2 18.6 %gather_fusion = bf16[4096,512]{1,0:T(8,128)(2,1)} fusion(bf16[512,512]{1,0:T(8,128)(2,1)} %param.9, s32[4096]{0:T(1024)S(1)} %get-tuple-element.12), kind=kCustom, calls=%fused_computation.2 | custom fusion | bytes 8404992 | tf_op jit(solution)/shard_map/jit(_take)/gather | solution.py:52
  79.8 3.9 %copy_select_fusion.1 = bf16[8,8,64,512]{3,2,0,1:T(8,128)(2,1)} fusion(bf16[8,8,64,512]{3,2,1,0:T(8,128)(2,1)} %bitcast.65, pred[8,8,64]{2,0,1:T(8,128)(4,1)S(1)} %copy.47), kind=kLoop, calls=%fused_computation.29 | loop fusion | flops 2097152 | bytes 8392704 | tf_op jit(solution)/shard_map/jit(_take)/select_n | solution.py:52
  83.7 4.3 %all-to-all-start = ((bf16[8,8,64,512]{3,2,0,1:T(8,128)(2,1)}), bf16[8,8,64,512]{3,2,0,1:T(8,128)(2,1)}, u32[]{:S(2)}, u32[]{:S(2)}) async-start(bf16[8,8,64,512]{3,2,0,1:T(8,128)(2,1)} %copy_select_fusion.1), calls=%async_computation | async-start | bytes 8388608 | tf_op jit(solution)/shard_map/all_to_all | solution.py:40
  94.0 20.2 %gather_fusion.1 = bf16[4096,512]{1,0:T(8,128)(2,1)} fusion(bf16[4096,512]{1,0:T(8,128)(2,1)} %fusion, s32[4096]{0:T(1024)S(1)} %get-tuple-element.11), kind=kCustom, calls=%fused_computation.3 | custom fusion | bytes 8404992 | tf_op jit(solution)/shard_map/jit(_take)/gather | solution.py:63
  114.1 3.9 %copy_select_fusion = bf16[8,8,64,512]{3,2,0,1:T(8,128)(2,1)} fusion(bf16[8,8,64,512]{3,2,1,0:T(8,128)(2,1)} %bitcast.64, pred[8,8,64]{2,0,1:T(8,128)(4,1)S(1)} %copy.52), kind=kLoop, calls=%fused_computation.28 | loop fusion | flops 2097152 | bytes 8392704 | tf_op jit(solution)/shard_map/jit(_take)/select_n | solution.py:63
  118.1 19.2 %all-to-all-done = bf16[8,8,64,512]{3,2,0,1:T(8,128)(2,1)} async-done(((bf16[8,8,64,512]{3,2,0,1:T(8,128)(2,1)}), bf16[8,8,64,512]{3,2,0,1:T(8,128)(2,1)}, u32[]{:S(2)}, u32[]{:S(2)}) %all-to-all-start) | async-done | bytes 4194336 | tf_op jit(solution)/shard_map/all_to_all | solution.py:40
  137.3 3.5 all-to-all-start.2
  145.6 4.0 %convolution_convert_fusion.2 = bf16[8,512,384]{2,1,0:T(8,128)(2,1)} fusion(bf16[8,512,512]{2,1,0:T(8,128)(2,1)S(1)} %bitcast.66, bf16[8,512,384]{2,1,0:T(8,128)(2,1)S(1)} %copy-done.12), kind=kOutput, calls=%fused_computation.33 | convolution fusion | flops 1612185600 | bytes 10485760 | tf_op jit(solution)/shard_map/lmd,ldf->lmf/dot_general | solution.py:55
  149.6 40.0 %all-to-all-done.2 = bf16[8,8,64,512]{3,2,0,1:T(8,128)(2,1)} async-done(((bf16[8,8,64,512]{3,2,0,1:T(8,128)(2,1)}), bf16[8,8,64,512]{3,2,0,1:T(8,128)(2,1)}, u32[]{:S(2)}, u32[]{:S(2)}) %all-to-all-start.2) | async-done | bytes 4194336 | tf_op jit(solution)/shard_map/all_to_all | solution.py:40
  197.3 5.3 %fusion.8 = (bf16[8,512,384]{2,1,0:T(8,128)(2,1)}, bf16[8,512,384]{2,1,0:T(8,128)(2,1)S(1)}) fusion(bf16[8,512,384]{2,1,0:T(8,128)(2,1)S(1)} %copy-done.13, bf16[8,512,384]{2,1,0:T(8,128)(2,1)S(1)} %convolution_convert_fusion.1, bf16[8,512,512]{2,1,0:T(8,128)(2,1)S(1)} %bitcast.68, bf16[8,512,384]{2,1,0:T(8,128)(2,1)S(1)} %copy-done), kind=kOutput, calls=%fused_computation.22 | convolution fusion | flops 1634205696 | bytes 19922944 | tf_op jit(solution)/shard_map/lmd,ldf->lmf/dot_general | solution.py:54
  210.9 7.5 %fusion.41 = f32[8,512,512]{2,1,0:T(8,128)} fusion(bf16[8,512,384]{2,1,0:T(8,128)(2,1)} %get-tuple-element.13, bf16[8,512,384]{2,1,0:T(8,128)(2,1)S(1)} %copy-done), kind=kOutput, calls=%fused_computation.89 | convolution fusion | flops 1610612736 | bytes 14680064 | tf_op jit(solution)/shard_map/lmf,ldf->lmd/dot_general | solution.py:70
  218.4 8.8 %add_convert_fusion = bf16[8,512,512]{2,1,0:T(8,128)(2,1)S(1)} fusion(f32[8,512,512]{2,1,0:T(8,128)} %fusion.41, bf16[8,512,384]{2,1,0:T(8,128)(2,1)} %param.13, bf16[8,512,384]{2,1,0:T(8,128)(2,1)} %copy-done.15, bf16[8,512,384]{2,1,0:T(8,128)(2,1)} %copy-done.17), kind=kOutput, calls=%fused_computation.11 | convolution fusion | flops 1627389952 | bytes 22020096 | tf_op jit(solution)/shard_map/lmf,ldf->lmd/dot_general | solution.py:70
  229.5 30.2 %all-to-all-done.1 = bf16[8,8,64,512]{3,2,0,1:T(8,128)(2,1)} async-done(((bf16[8,8,64,512]{3,2,0,1:T(8,128)(2,1)}), bf16[8,8,64,512]{3,2,0,1:T(8,128)(2,1)}, u32[]{:S(2)}, u32[]{:S(2)}) %all-to-all-start.1) | async-done | bytes 4194336 | tf_op jit(solution)/shard_map/all_to_all | solution.py:40
  259.7 3.5 %all-to-all-start.3 = ((bf16[8,8,64,512]{3,2,0,1:T(8,128)(2,1)}), bf16[8,8,64,512]{3,2,0,1:T(8,128)(2,1)}, u32[]{:S(2)}, u32[]{:S(2)}) async-start(bf16[8,8,64,512]{3,2,0,1:T(8,128)(2,1)} %copy.56), calls=%async_computation.3 | async-start | bytes 8388608 | tf_op jit(solution)/shard_map/all_to_all | solution.py:40
  263.2 7.4 %fusion.42 = f32[8,512,384]{2,1,0:T(8,128)} fusion(bf16[8,512,512]{2,1,0:T(8,128)(2,1)} %bitcast.67, bf16[8,512,384]{2,1,0:T(8,128)(2,1)S(1)} %copy-done.5), kind=kOutput, calls=%fused_computation.90 | convolution fusion | flops 1610612736 | bytes 13631488 | tf_op jit(solution)/shard_map/lmd,lmf->ldf/dot_general | solution.py:68
  270.7 5.3 %fusion.38 = f32[8,384,512]{2,1,0:T(8,128)} fusion(bf16[8,512,512]{2,1,0:T(8,128)(2,1)S(1)} %bitcast.71, bf16[8,512,384]{2,1,0:T(8,128)(2,1)S(1)} %copy-done.14, bf16[8,512,384]{2,1,0:T(8,128)(2,1)S(1)} %copy-done.18), kind=kOutput, calls=%fused_computation.88 | convolution fusion | flops 1623195648 | bytes 16777216 | tf_op jit(solution)/shard_map/lmf,lmd->lfd/dot_general | solution.py:67
  276.0 5.8 %fusion.35 = f32[8,512,384]{2,1,0:T(8,128)} fusion(bf16[8,512,512]{2,1,0:T(8,128)(2,1)S(1)} %bitcast.69, bf16[8,512,384]{2,1,0:T(8,128)(2,1)S(1)} %copy-done.16, bf16[8,512,384]{2,1,0:T(8,128)(2,1)S(1)} %copy-done.18), kind=kOutput, calls=%fused_computation.87 | convolution fusion | flops 1623195648 | bytes 16777216 | tf_op jit(solution)/shard_map/lmd,lmf->ldf/dot_general | solution.py:69
  281.7 4.6 %copy.51 = bf16[8,8,64,512]{3,2,1,0:T(8,128)(2,1)} copy(bf16[8,8,64,512]{3,2,0,1:T(8,128)(2,1)} %all-to-all-done.1) | data formatting | bytes 8388608 | tf_op jit(solution)/shard_map/all_to_all | solution.py:40
  286.3 20.1 %gather_fusion.2 = bf16[4096,512]{1,0:T(8,128)(2,1)} fusion(bf16[4096,512]{1,0:T(8,128)(2,1)} %bitcast.63, s32[4096]{0:T(1024)S(1)} %broadcast_clamp_fusion), kind=kCustom, calls=%fused_computation.clone | custom fusion | bytes 8404992 | tf_op jit(solution)/shard_map/jit(_take)/gather | solution.py:59
  311.9 4.7 %copy.57 = bf16[8,8,64,512]{3,2,1,0:T(8,128)(2,1)} copy(bf16[8,8,64,512]{3,2,0,1:T(8,128)(2,1)} %all-to-all-done.3) | data formatting | bytes 8388608 | tf_op jit(solution)/shard_map/all_to_all | solution.py:40
  316.6 20.1 %gather_fusion.3 = bf16[4096,512]{1,0:T(8,128)(2,1)} fusion(bf16[4096,512]{1,0:T(8,128)(2,1)} %bitcast.62, s32[4096]{0:T(1024)S(1)} %broadcast_clamp_fusion), kind=kCustom, calls=%fused_computation.1.clone | custom fusion | bytes 8404992 | tf_op jit(solution)/shard_map/jit(_take)/gather | solution.py:72
  336.7 7.0 %bitcast_reduce_fusion = bf16[512,512]{1,0:T(8,128)(2,1)} fusion(bf16[4096,512]{1,0:T(8,128)(2,1)} %gather_fusion.3, pred[4096]{0:T(1024)(128)(4,1)S(1)} %get-tuple-element.7), kind=kLoop, calls=%fused_computation.23 | loop fusion | flops 3932160 | bytes 4722688 | tf_op jit(solution)/shard_map/reduce_sum | solution.py:73
  (75 shorter events, 48.3 us)
Async XLA Ops:
  0.6 195.8 %copy-start = (bf16[8,512,384]{2,1,0:T(8,128)(2,1)S(1)}, bf16[8,512,384]{2,1,0:T(8,128)(2,1)}, u32[]{:S(2)}) copy-start(bf16[8,512,384]{2,1,0:T(8,128)(2,1)} %param.12) | copy-start | bytes 9437188
  83.7 6.5 %copy-start.10 = (f32[512,8]{0,1:T(8,128)S(1)}, f32[512,8]{0,1:T(8,128)}, u32[]{:S(2)}) copy-start(f32[512,8]{0,1:T(8,128)} %param.11) | copy-start | bytes 49156
  83.7 53.5 %all-to-all-start = ((bf16[8,8,64,512]{3,2,0,1:T(8,128)(2,1)}), bf16[8,8,64,512]{3,2,0,1:T(8,128)(2,1)}, u32[]{:S(2)}, u32[]{:S(2)}) async-start(bf16[8,8,64,512]{3,2,0,1:T(8,128)(2,1)} %copy_select_fusion.1), calls=%async_computation | async-start | bytes 8388608 | tf_op jit(solution)/shard_map/all_to_all | solution.py:40
  137.3 52.3 %all-to-all-start.2 = ((bf16[8,8,64,512]{3,2,0,1:T(8,128)(2,1)}), bf16[8,8,64,512]{3,2,0,1:T(8,128)(2,1)}, u32[]{:S(2)}, u32[]{:S(2)}) async-start(bf16[8,8,64,512]{3,2,0,1:T(8,128)(2,1)} %copy_select_fusion), calls=%async_computation.2 | async-start | bytes 8388608 | tf_op jit(solution)/shard_map/all_to_all | solution.py:40
  140.7 4.9 %copy-start.12 = (bf16[8,512,384]{2,1,0:T(8,128)(2,1)S(1)}, bf16[8,512,384]{2,1,0:T(8,128)(2,1)}, u32[]{:S(2)}) copy-start(bf16[8,512,384]{2,1,0:T(8,128)(2,1)} %param.13) | copy-start | bytes 9437188
  143.6 2.0 copy-start.2
  189.6 4.6 %copy-start.11 = (bf16[8,384,512]{2,1,0:T(8,128)(2,1)S(1)}, bf16[8,384,512]{2,1,0:T(8,128)(2,1)}, u32[]{:S(2)}) copy-start(bf16[8,384,512]{2,1,0:T(8,128)(2,1)} %param.14) | copy-start | bytes 9437188
  192.2 1.9 copy-start.7
  194.1 2.4 copy-start.3
  194.1 3.2 copy-start.13
  197.3 5.3 %copy-start.15 = (bf16[8,512,384]{2,1,0:T(8,128)(2,1)}, bf16[8,512,384]{2,1,0:T(8,128)(2,1)S(1)}, u32[]{:S(2)}) copy-start(bf16[8,512,384]{2,1,0:T(8,128)(2,1)S(1)} %convolution_convert_fusion.1) | copy-start | bytes 9437188
  202.6 2.4 copy-start.17
  207.3 52.3 %all-to-all-start.1 = ((bf16[8,8,64,512]{3,2,0,1:T(8,128)(2,1)}), bf16[8,8,64,512]{3,2,0,1:T(8,128)(2,1)}, u32[]{:S(2)}, u32[]{:S(2)}) async-start(bf16[8,8,64,512]{3,2,0,1:T(8,128)(2,1)} %copy.50), calls=%async_computation.1 | async-start | bytes 8388608 | tf_op jit(solution)/shard_map/all_to_all | solution.py:40
  229.5 33.7 %copy-start.5 = (bf16[8,512,384]{2,1,0:T(8,128)(2,1)S(1)}, bf16[8,512,384]{2,1,0:T(8,128)(2,1)}, u32[]{:S(2)}) copy-start(bf16[8,512,384]{2,1,0:T(8,128)(2,1)} %get-tuple-element.13) | copy-start | bytes 9437188
  259.7 52.3 %all-to-all-start.3 = ((bf16[8,8,64,512]{3,2,0,1:T(8,128)(2,1)}), bf16[8,8,64,512]{3,2,0,1:T(8,128)(2,1)}, u32[]{:S(2)}, u32[]{:S(2)}) async-start(bf16[8,8,64,512]{3,2,0,1:T(8,128)(2,1)} %copy.56), calls=%async_computation.3 | async-start | bytes 8388608 | tf_op jit(solution)/shard_map/all_to_all | solution.py:40
  263.2 7.5 %copy-start.8 = (bf16[8,8,64,512]{3,2,1,0:T(8,128)(2,1)S(1)}, bf16[8,8,64,512]{3,2,1,0:T(8,128)(2,1)}, u32[]{:S(2)}) copy-start(bf16[8,8,64,512]{3,2,1,0:T(8,128)(2,1)} %copy-done.7) | copy-start | bytes 12582916
  263.2 7.5 %copy-start.14 = (bf16[8,512,384]{2,1,0:T(8,128)(2,1)S(1)}, bf16[8,512,384]{2,1,0:T(8,128)(2,1)}, u32[]{:S(2)}) copy-start(bf16[8,512,384]{2,1,0:T(8,128)(2,1)} %convolution_convert_fusion.2) | copy-start | bytes 9437188
  263.2 7.4 %copy-start.18 = (bf16[8,512,384]{2,1,0:T(8,128)(2,1)S(1)}, bf16[8,512,384]{2,1,0:T(8,128)(2,1)}, u32[]{:S(2)}) copy-start(bf16[8,512,384]{2,1,0:T(8,128)(2,1)} %copy-done.17) | copy-start | bytes 9437188
  270.6 5.3 %copy-start.4 = (bf16[8,8,64,512]{3,2,1,0:T(8,128)(2,1)S(1)}, bf16[8,8,64,512]{3,2,1,0:T(8,128)(2,1)}, u32[]{:S(2)}) copy-start(bf16[8,8,64,512]{3,2,1,0:T(8,128)(2,1)} %copy-done.2) | copy-start | bytes 12582916
  270.7 5.3 %copy-start.16 = (bf16[8,512,384]{2,1,0:T(8,128)(2,1)S(1)}, bf16[8,512,384]{2,1,0:T(8,128)(2,1)}, u32[]{:S(2)}) copy-start(bf16[8,512,384]{2,1,0:T(8,128)(2,1)} %copy-done.15) | copy-start | bytes 9437188
  336.7 7.0 %copy-start.6 = (bf16[4096,512]{1,0:T(8,128)(2,1)S(1)}, bf16[4096,512]{1,0:T(8,128)(2,1)}, u32[]{:S(2)}) copy-start(bf16[4096,512]{1,0:T(8,128)(2,1)} %gather_fusion.2) | copy-start | bytes 12582916
  336.7 7.0 %copy-start.9 = (bf16[512,512]{1,0:T(8,128)(2,1)S(1)}, bf16[512,512]{1,0:T(8,128)(2,1)}, u32[]{:S(2)}) copy-start(bf16[512,512]{1,0:T(8,128)(2,1)} %param.15) | copy-start | bytes 1572868
  343.7 4.2 %copy-start.1 = (bf16[8,512,384]{2,1,0:T(8,128)(2,1)S(1)}, bf16[8,512,384]{2,1,0:T(8,128)(2,1)}, u32[]{:S(2)}) copy-start(bf16[8,512,384]{2,1,0:T(8,128)(2,1)} %param.12) | copy-start | bytes 9437188
where the time goes:
time: 352 us; the launch traced here: 348 us
  local copies, waits for them, and re-layouts  127 us (36%)
  waiting for transfers between devices  90.6 us (26%)
  other arithmetic  59.7 us (17%)
  matrix products  55.5 us (16%)
  starting transfers between devices  14.6 us (4%)
    all_to_all x4, waiting for transfers between devices, exchange(): return lax.all_to_all(send_buf, EP_AXES, 1, 1, tiled=True)  90.6 us
    another operation x3, other arithmetic  37.1 us
    gather x1, local copies, waits for them, and re-layouts, local_step(): jnp.take(slot_grad, buf_slots, axis=0, mode='fill', fill_value=0)  20.2 us
    gather x1, local copies, waits for them, and re-layouts, local_step(): jnp.take(back_out.reshape(-1, model_dim), slot_dest, axis=0)  20.1 us
    gather x1, local copies, waits for them, and re-layouts, local_step(): jnp.take(back_g.reshape(-1, model_dim), slot_dest, axis=0)  20.1 us
    gather x1, local copies, waits for them, and re-layouts, local_step(): jnp.take(tokens, buf_slots // top_k, axis=0, mode='fill', fill_value=0)  18.6 us
    scatter x1, local copies, waits for them, and re-layouts, pack_slots(): jnp.full((experts * capacity,), slot_count, jnp.int32).at[slot_dest]  15.5 us
    all_to_all x4, local copies, waits for them, and re-layouts, exchange(): return lax.all_to_all(send_buf, EP_AXES, 1, 1, tiled=True)  14.7 us
  transfers between devices with their start and end apart: 4, of which 4 were waited for; matrix products, arithmetic and copies ran while one was open for 30% of the time, Pallas kernels for 0%

commit v1 on v0

v1 whole, which is shorter than its diff:
```python
import functools

import jax
import jax.numpy as jnp
from jax import lax
from jax.experimental import pallas as pl
from jax.experimental.pallas import tpu as pltpu
from jax.sharding import PartitionSpec as P

EP_AXES = ('row', 'col', 'core')
ALL_AXES = ('part', 'row', 'col', 'core')
MESH = pl.DeviceIdType.MESH
F32 = jnp.float32
BF16 = jnp.bfloat16
NT = (((1,), (1,)), ((), ()))
TN = (((0,), (0,)), ((), ()))

AG_X, AG_DY, RG, OX, PX, RS_O, RS_P, GG, N_SEM = 0, 10, 20, 27, 31, 35, 41, 47, 54


def dot(a, b):
    return jnp.dot(a, b, preferred_element_type=F32)


def dotg(a, b, dims):
    return lax.dot_general(a, b, dims, preferred_element_type=F32)


def kernel(T, D, FF, NE, CAP,
           x_ref, dy_ref, rg_ref, wg_ref, wu_ref, wd_ref,
           moe_ref, gx_ref, gg_ref, dwg_ref, dwu_ref, dwd_ref,
           xa, dya, xg, us, vs, os_, wg, wu, wd, acc, rd, fr, orv, prv,
           swg, swu, swd, pb, sb, rga, rm, gm, mb, rt, gt, gga, ggs,
           ssem, rsem, lsem):
    H = T // 2
    row, col, core = lax.axis_index('row'), lax.axis_index('col'), lax.axis_index('core')
    me = row * 4 + col * 2 + core
    partner = row * 4 + col * 2 + (1 - core)

    def dev(rel):
        return {
            'row': 1 - row if rel & 4 else row,
            'col': 1 - col if rel & 2 else col,
            'core': 1 - core if rel & 1 else core,
        }

    def rc(i, src, dst, rel):
        return pltpu.make_async_remote_copy(
            src_ref=src, dst_ref=dst, send_sem=ssem.at[i], recv_sem=rsem.at[i],
            device_id=dev(rel), device_id_type=MESH)

    def gather_copies(b, buf):
        lo, hi = pl.ds(0, H), pl.ds(H, H)
        return [
            rc(b + 0, buf.at[0], buf.at[1], 1),
            rc(b + 1, buf.at[0, hi], buf.at[2, hi], 2),
            rc(b + 2, buf.at[0, lo], buf.at[2, lo], 2),
            rc(b + 3, buf.at[0, lo], buf.at[4, lo], 4),
            rc(b + 4, buf.at[0, hi], buf.at[4, hi], 4),
            rc(b + 5, buf.at[2, hi], buf.at[6, hi], 4),
            rc(b + 6, buf.at[4, lo], buf.at[6, lo], 2),
            rc(b + 7, buf.at[2], buf.at[3], 1),
            rc(b + 8, buf.at[4], buf.at[5], 1),
            rc(b + 9, buf.at[6], buf.at[7], 1),
        ]

    lx = pltpu.make_async_copy(x_ref, xa.at[0], lsem.at[0])
    ldy = pltpu.make_async_copy(dy_ref, dya.at[0], lsem.at[1])
    lwg = pltpu.make_async_copy(wg_ref, wg, lsem.at[2])
    lwu = pltpu.make_async_copy(wu_ref, wu, lsem.at[3])
    lwd = pltpu.make_async_copy(wd_ref, wd, lsem.at[4])
    lx.start()
    ldy.start()
    lwg.start()
    lwu.start()
    lwd.start()

    barrier = pltpu.get_barrier_semaphore()
    for rel in range(1, 8):
        pl.semaphore_signal(barrier, inc=1, device_id=dev(rel), device_id_type=MESH)
    pl.semaphore_wait(barrier, 7)

    rgc = [rc(RG + rel - 1, rg_ref, rga.at[rel], rel) for rel in range(1, 8)]
    for c in rgc:
        c.start()
    cx = gather_copies(AG_X, xa)
    cy = gather_copies(AG_DY, dya)
    lx.wait()
    for i in (1, 3, 0, 2, 4):
        cx[i].start()

    rga[0] = rg_ref[...]

    i0 = lax.broadcasted_iota(jnp.int32, (T, T), 0)
    i1 = lax.broadcasted_iota(jnp.int32, (T, T), 1)
    sb[0] = (i0 < i1).astype(F32).astype(BF16)
    sb[1] = (i0 > i1).astype(F32).astype(BF16)
    sb[2] = (i0 == i1).astype(F32).astype(BF16)
    for c in rgc:
        c.wait_recv()
    mb[...] = jnp.zeros_like(mb)
    gm[...] = jnp.zeros_like(gm)
    sub = lax.broadcasted_iota(jnp.int32, (NE, T), 0)
    for idx in range(12):
        src = idx if idx < 8 else 2 * (idx - 8)
        owner = me if idx < 8 else partner
        ids = (sub + owner * NE).astype(F32)
        hits = jnp.zeros((NE, T), F32)
        gates = jnp.zeros((NE, T), F32)
        for j in range(8):
            hit = rga[src, j:j + 1, :] == ids
            hits = hits + jnp.where(hit, 1.0, 0.0)
            gates = gates + jnp.where(hit, rga[src, 8 + j:9 + j, :], 0.0)
        mb[idx] = hits
        gm[idx] = gates
    m_all = mb[...].reshape(16 * NE, T)
    m_bf = m_all.astype(BF16)
    ranks = dot(m_bf, sb[0])
    rm[...] = jnp.where(m_all > 0.5, ranks, -1.0).reshape(16, NE, T)
    m_t = dotg(sb[2], m_bf, NT)
    r_t = dotg(sb[1], m_bf, NT)
    rt[...] = jnp.where(m_t > 0.5, r_t, -1.0).astype(BF16)
    g_all = gm[...].reshape(16 * NE, T)
    g_hi = g_all.astype(BF16)
    rest = g_all - g_hi.astype(F32)
    g_mid = rest.astype(BF16)
    g_lo = (rest - g_mid.astype(F32)).astype(BF16)
    for k, piece in enumerate((g_hi, g_mid, g_lo)):
        gt[k] = dotg(sb[2], piece, NT).astype(BF16)

    lane_r = lax.broadcasted_iota(jnp.int32, (CAP, T), 0).astype(F32)

    def build_p(d):
        r_d = rm[d]
        for l in range(NE):
            pb[l * CAP:(l + 1) * CAP, :] = jnp.where(lane_r == r_d[l:l + 1, :], 1.0, 0.0).astype(BF16)

    def gather_x(d):
        build_p(d)
        xg[d] = dot(pb[...], xa[d]).astype(BF16).reshape(NE, CAP, D)

    def gather_x_loop(first, step, count):
        def one(i, carry):
            gather_x(first + step * i)
            return carry
        lax.fori_loop(0, count, one, 0)

    cx[0].wait_recv()
    gather_x_loop(0, 1, 2)
    cx[1].wait_recv()
    cx[5].start()
    cx[3].wait_recv()
    cx[6].start()
    cx[2].wait_recv()
    cx[7].start()
    cx[4].wait_recv()
    cx[8].start()
    ldy.wait()
    for i in (1, 3, 0, 2, 4):
        cy[i].start()
    gather_x_loop(2, 2, 2)
    cx[7].wait_recv()
    cx[8].wait_recv()
    gather_x_loop(3, 2, 2)
    cx[5].wait_recv()
    cx[6].wait_recv()
    cx[9].start()
    gather_x_loop(6, 1, 1)
    cx[9].wait_recv()
    gather_x_loop(7, 1, 1)

    lwg.wait()
    lwu.wait()
    lwd.wait()

    def forward(l, carry):
        rows = xg[:, pl.ds(l, 1)].reshape(T, D)
        u = dot(rows, wg[l]).astype(BF16)
        v = dot(rows, wu[l]).astype(BF16)
        us[l] = u
        vs[l] = v
        uf = u.astype(F32)
        h = (uf * jax.nn.sigmoid(uf) * v.astype(F32)).astype(BF16)
        o = dot(h, wd[l]).astype(BF16)
        os_[:, pl.ds(l, 1)] = o.reshape(8, 1, CAP, D)
        return carry

    lax.fori_loop(0, NE, forward, 0)

    cy[1].wait_recv()
    cy[5].start()
    cy[3].wait_recv()
    cy[6].start()
    cy[2].wait_recv()
    cy[7].start()
    cy[4].wait_recv()
    cy[8].start()

    order = (3, 1, 2, 0)

    def swap_copies(b, buf):
        return {h: rc(b + h, os_.at[2 * h + 1], buf.at[h], 1) for h in range(4)}

    def reduce_copies(b, k):
        lo, hi = pl.ds(0, H), pl.ds(H, H)
        return [
            rc(b + 0, acc.at[k, 3, lo], rd.at[k, 0], 2),
            rc(b + 1, acc.at[k, 3, hi], rd.at[k, 1], 4),
            rc(b + 2, acc.at[k, 1, lo], fr.at[k, 0, lo], 2),
            rc(b + 3, acc.at[k, 2, hi], fr.at[k, 1, hi], 4),
            rc(b + 4, acc.at[k, 1, hi], fr.at[k, 0, hi], 2),
            rc(b + 5, acc.at[k, 2, lo], fr.at[k, 1, lo], 4),
        ]

    e0 = lax.broadcasted_iota(jnp.int32, (16 * NE, T), 0)
    e1 = lax.broadcasted_iota(jnp.int32, (16 * NE, T), 1) // CAP
    rank_lane = lax.rem(lax.broadcasted_iota(jnp.int32, (T, T), 1), CAP).astype(F32)

    def spread(idx, rows, weighted):
        pick = jnp.where(e0 == e1 + idx * NE, 1.0, 0.0).astype(BF16)
        hit = dot(rt[...], pick) == rank_lane
        if weighted:
            for k in range(3):
                sb[k] = jnp.where(hit, dot(gt[k], pick), 0.0).astype(BF16)
            return dot(sb[0], rows) + dot(sb[1], rows) + dot(sb[2], rows)
        sb[0] = jnp.where(hit, 1.0, 0.0).astype(BF16)
        return dot(sb[0], rows)

    def combine(k, h, recv, weighted):
        a = spread(2 * h, os_[2 * h].reshape(T, D), weighted)
        acc[k, h] = a + spread(8 + h, recv[h].reshape(T, D), weighted)

    ox = swap_copies(OX, orv)
    ro = reduce_copies(RS_O, 0)
    for h in order:
        ox[h].start()
    for h in order:
        ox[h].wait_recv()

    def combine_all(k, recv, copies, weighted):
        def one(i, carry):
            h = 3 - i
            combine(k, h, recv, weighted)

            @pl.when(i == 0)
            def _():
                copies[0].start()
                copies[1].start()

            @pl.when(i == 1)
            def _():
                copies[3].start()

            @pl.when(i == 2)
            def _():
                copies[2].start()
            return carry
        lax.fori_loop(0, 4, one, 0)

    combine_all(0, orv, ro, True)

    cy[5].wait_recv()
    cy[6].wait_recv()
    cy[9].start()
    cy[0].wait_recv()
    cy[7].wait_recv()
    cy[8].wait_recv()
    cy[9].wait_recv()
    for c in cx:
        c.wait_send()

    ggc = [rc(GG + rel - 1, ggs.at[rel], gga.at[rel], rel) for rel in range(1, 8)]

    def gather_dy(d, carry):
        build_p(d)
        rows = dot(pb[...], dya[d])
        outs = os_[d].reshape(T, D).astype(F32)
        gg_rows = jnp.sum(rows * outs, axis=1, keepdims=True)
        r_d = rm[d]
        g_d = gm[d]
        for l in range(NE):
            hit = lane_r == r_d[l:l + 1, :]
            gcol = jnp.sum(jnp.where(hit, g_d[l:l + 1, :], 0.0), axis=1, keepdims=True)
            xa[d, l * CAP:(l + 1) * CAP, :] = (gcol * rows[l * CAP:(l + 1) * CAP, :]).astype(BF16)
            ggs[d, l:l + 1, :] = jnp.sum(
                jnp.where(hit, gg_rows[l * CAP:(l + 1) * CAP, :], 0.0), axis=0, keepdims=True)
        return carry

    lax.fori_loop(0, 8, gather_dy, 0)
    for c in ggc:
        c.start()
    for h in order:
        ox[h].wait_send()

    def finish_grads(l):
        return [
            pltpu.make_async_copy(swg, dwg_ref.at[l], lsem.at[5]),
            pltpu.make_async_copy(swu, dwu_ref.at[l], lsem.at[6]),
            pltpu.make_async_copy(swd, dwd_ref.at[l], lsem.at[7]),
        ]

    def backward(l, carry):
        rows = xg[:, pl.ds(l, 1)].reshape(T, D)
        c = xa[:, pl.ds(pl.multiple_of(l * CAP, CAP), CAP), :].reshape(T, D)
        dh = dotg(c, wd[l], NT).astype(BF16).astype(F32)
        uf = us[l].astype(F32)
        vf = vs[l].astype(F32)
        s = jax.nn.sigmoid(uf)
        sl = uf * s
        h = (sl * vf).astype(BF16)
        dv = (dh * sl).astype(BF16)
        du = (dh * vf * (s + sl * (1.0 - s))).astype(BF16)
        pr = (dotg(du, wg[l], NT) + dotg(dv, wu[l], NT)).astype(BF16)
        os_[:, pl.ds(l, 1)] = pr.reshape(8, 1, CAP, D)

        @pl.when(l > 0)
        def _():
            for cp in finish_grads(l - 1):
                cp.wait()
        swd[...] = dotg(h, c, TN)
        swg[...] = dotg(rows, du, TN)
        swu[...] = dotg(rows, dv, TN)
        for cp in finish_grads(l):
            cp.start()
        return carry

    def pass_on(k, copies):
        copies[0].wait_recv()
        acc[k, 2, :H] = acc[k, 2, :H] + rd[k, 0]
        copies[5].start()
        copies[1].wait_recv()
        acc[k, 1, H:] = acc[k, 1, H:] + rd[k, 1]
        copies[4].start()

    def finish(k, copies, out):
        for i in (2, 3, 4, 5):
            copies[i].wait_recv()
        out[...] = (acc[k, 0] + fr[k, 0] + fr[k, 1]).astype(BF16)

    lax.fori_loop(0, NE // 2, backward, 0)
    pass_on(0, ro)
    lax.fori_loop(NE // 2, NE, backward, 0)

    px = swap_copies(PX, prv)
    rp = reduce_copies(RS_P, 1)
    for h in order:
        px[h].start()
    for h in order:
        px[h].wait_recv()
    combine_all(1, prv, rp, False)

    for c in ggc:
        c.wait_recv()
    gga[0] = ggs[0]
    out = [jnp.zeros((1, T), F32) for _ in range(8)]
    for rel in range(8):
        d = dev(rel)
        base = d['row'] * 4 + d['col'] * 2 + d['core']
        ids = (sub + base * NE).astype(F32)
        part = gga[rel]
        for j in range(8):
            hit = rg_ref[j:j + 1, :] == ids
            out[j] = out[j] + jnp.sum(jnp.where(hit, part, 0.0), axis=0, keepdims=True)
    for j in range(8):
        gg_ref[j:j + 1, :] = out[j]

    finish(0, ro, moe_ref)
    pass_on(1, rp)
    finish(1, rp, gx_ref)

    for cp in finish_grads(NE - 1):
        cp.wait()
    for c in rgc + cy + ggc + ro + rp + [px[h] for h in order]:
        c.wait_send()


def solution(mesh):
    tok_spec = P(ALL_AXES, None)
    w_spec = P(EP_AXES, None, None)
    gw_spec = P(ALL_AXES, None, None)

    def local_step(tokens, route_idx, gate_vals, w_gate, w_up, w_down, grad_out):
        T, K = route_idx.shape
        D = tokens.shape[1]
        NE, _, FF = w_gate.shape
        CAP = T * K // (8 * NE)
        rg = jnp.concatenate([route_idx.astype(F32).T, gate_vals.T], axis=0)
        vm = pl.BlockSpec(memory_space=pltpu.VMEM)
        hbm = pl.BlockSpec(memory_space=pl.ANY)
        sds = jax.ShapeDtypeStruct
        outs = pl.pallas_call(
            functools.partial(kernel, T, D, FF, NE, CAP),
            out_shape=(sds((T, D), BF16), sds((T, D), BF16), sds((K, T), F32),
                       sds((NE, D, FF), F32), sds((NE, D, FF), F32), sds((NE, FF, D), F32)),
            in_specs=[hbm, hbm, vm, hbm, hbm, hbm],
            out_specs=(vm, vm, vm, hbm, hbm, hbm),
            scratch_shapes=[
                pltpu.VMEM((8, T, D), BF16),
                pltpu.VMEM((8, T, D), BF16),
                pltpu.VMEM((8, NE, CAP, D), BF16),
                pltpu.VMEM((NE, T, FF), BF16),
                pltpu.VMEM((NE, T, FF), BF16),
                pltpu.VMEM((8, NE, CAP, D), BF16),
                pltpu.VMEM((NE, D, FF), BF16),
                pltpu.VMEM((NE, D, FF), BF16),
                pltpu.VMEM((NE, FF, D), BF16),
                pltpu.VMEM((2, 4, T, D), F32),
                pltpu.VMEM((2, 2, T // 2, D), F32),
                pltpu.VMEM((2, 2, T, D), F32),
                pltpu.VMEM((4, NE, CAP, D), BF16),
                pltpu.VMEM((4, NE, CAP, D), BF16),
                pltpu.VMEM((D, FF), F32),
                pltpu.VMEM((D, FF), F32),
                pltpu.VMEM((FF, D), F32),
                pltpu.VMEM((T, T), BF16),
                pltpu.VMEM((3, T, T), BF16),
                pltpu.VMEM((8, 2 * K, T), F32),
                pltpu.VMEM((16, NE, T), F32),
                pltpu.VMEM((16, NE, T), F32),
                pltpu.VMEM((16, NE, T), F32),
                pltpu.VMEM((T, 16 * NE), BF16),
                pltpu.VMEM((3, T, 16 * NE), BF16),
                pltpu.VMEM((8, NE, T), F32),
                pltpu.VMEM((8, NE, T), F32),
                pltpu.SemaphoreType.DMA((N_SEM,)),
                pltpu.SemaphoreType.DMA((N_SEM,)),
                pltpu.SemaphoreType.DMA((8,)),
            ],
            compiler_params=pltpu.CompilerParams(
                collective_id=0, has_side_effects=True, vmem_limit_bytes=67043328),
        )(tokens, grad_out, rg, w_gate, w_up, w_down)
        moe, gx, gg, dwg, dwu, dwd = outs
        return moe, gx, gg.T, dwg, dwu, dwd

    return jax.shard_map(
        local_step, mesh=mesh,
        in_specs=(tok_spec, tok_spec, tok_spec, w_spec, w_spec, w_spec, tok_spec),
        out_specs=(tok_spec, tok_spec, tok_spec, gw_spec, gw_spec, gw_spec),
        check_vma=False)
```

time: 352 us -> 143 us (0.41); the launches traced: 348 us -> 143 us
  Pallas kernels: 0 us -> 121 us
  local copies, waits for them, and re-layouts: 127 us -> 18.9 us
  waiting for transfers between devices: 90.6 us -> 0 us
  other arithmetic: 59.7 us -> 2.05 us
  matrix products: 55.5 us -> 0 us
  starting transfers between devices: 14.6 us -> 0 us
    pallas_call x0 -> x1, Pallas kernels: none -> 121 us  [local_step(): pl.pallas_call(functools.partial(kernel, T, D, FF, NE, CAP), out_shape=(s...]
    all_to_all x4 -> x0, waiting for transfers between devices: 90.6 us -> none  [exchange(): return lax.all_to_all(send_buf, EP_AXES, 1, 1, tiled=True)]
    gather x4 -> x0, local copies, waits for them, and re-layouts: 79 us -> none  [the longest x1 20.2 us: local_step(): jnp.take(slot_grad, buf_slots, axis=0, mode='fill', fill_value=0)]
    dot_general x11 -> x0, matrix products: 55.5 us -> none  [the longest x1 8.77 us: local_step(): jnp.einsum('lmf,ldf->lmd', d_up_h, w_up, preferred_element_type=jnp.float32)]
    another operation x3 -> x0, other arithmetic: 37.1 us -> none
    scatter x1 -> x0, local copies, waits for them, and re-layouts: 15.5 us -> none  [pack_slots(): jnp.full((experts * capacity,), slot_count, jnp.int32).at[slot_dest]]
    all_to_all x4 -> x0, local copies, waits for them, and re-layouts: 14.7 us -> none  [exchange(): return lax.all_to_all(send_buf, EP_AXES, 1, 1, tiled=True)]
    all_to_all x4 -> x0, starting transfers between devices: 14.6 us -> none  [exchange(): return lax.all_to_all(send_buf, EP_AXES, 1, 1, tiled=True)]
  transfers between devices with their start and end apart: 4 -> 0, of which waited for: 4 -> 0; matrix products, arithmetic and copies ran while one was open for 30% -> 0% of each run, Pallas kernels for 0% -> 0%
where the time goes in v1:
time: 143 us
  Pallas kernels  121 us (85%)
  local copies, waits for them, and re-layouts  18.9 us (13%)
  other arithmetic  2.05 us (1%)
    pallas_call x1, Pallas kernels, local_step(): pl.pallas_call(functools.partial(kernel, T, D, FF, NE, CAP), out_shape=(s...  121 us
    unnamed x12, local copies, waits for them, and re-layouts  18.9 us

profile of v1, /device:TPU:0, one launch (start us, length us, event | category | flops | bytes accessed | tf_op | source)
XLA Modules:
  0.0 143.0 jit_solution(4021895689718571472)
XLA Ops:
  0.6 0.7 convert_bitcast_fusion
  1.4 1.3 pad_maximum_fusion.rg_ref
  2.7 121.4 %shard_map.118 = (bf16[512,512]{1,0:T(8,128)(2,1)}, bf16[512,512]{1,0:T(8,128)(2,1)}, f32[8,512]{1,0:T(8,128)}, f32[8,512,384]{2,1,0:T(8,128)}, f32[8,512,384]{2,1,0:T(8,128)}, /*index=5*/f32[8,384,512]{2,1,0:T(8,128)}) custom-call(bf16[512,512]{1,0:T(8,128)(2,1)} %x_ref.1, bf16[512,512]{1,0:T(8,128)(2,1)} %dy_ref.1, f32[16,512]{1,0:T(8,128)} %pad_maximum_fusion.rg_ref, ...), custom_call_target="tpu_custom_call" | custom-call | tf_op jit(solution)/shard_map/pallas_call | solution.py:391
  124.1 1.9 %copy.19 = bf16[512,512]{1,0:T(8,128)(2,1)} copy(bf16[512,512]{1,0:T(8,128)(2,1)} %get-tuple-element.24) | data formatting | bytes 1048576
  126.0 1.9 %copy.20 = bf16[512,512]{1,0:T(8,128)(2,1)} copy(bf16[512,512]{1,0:T(8,128)(2,1)} %get-tuple-element.25) | data formatting | bytes 1048576
  127.8 1.3 copy.21
  129.2 0.0 copy-start
  129.2 0.0 slice-start
  129.2 6.6 %copy.22 = f32[8,512,384]{2,1,0:T(8,128)} copy(f32[8,512,384]{2,1,0:T(8,128)} %get-tuple-element.27) | data formatting | bytes 12582912
  135.8 0.0 copy-done
  135.8 0.0 slice-start.1
  135.8 3.2 %copy.23 = f32[8,512,384]{2,1,0:T(8,128)} copy(f32[8,512,384]{2,1,0:T(8,128)S(1)} %copy-done) | data formatting | bytes 12582912
  139.0 0.0 slice-done
  139.0 1.3 slice-done.1
  140.3 2.7 %copy.24 = f32[8,384,512]{2,1,0:T(8,128)} copy(f32[8,384,512]{2,1,0:T(8,128)S(1)} %bitcast.5) | data formatting | bytes 12582912
  (1 shorter events, 0.0 us)
Async XLA Ops:
  129.2 6.6 %copy-start = (f32[8,512,384]{2,1,0:T(8,128)S(1)}, f32[8,512,384]{2,1,0:T(8,128)}, u32[]{:S(2)}) copy-start(f32[8,512,384]{2,1,0:T(8,128)} %get-tuple-element.28) | copy-start | bytes 18874372
  129.2 9.8 %slice-start = ((s8[6291456]{0:T(1024)(128)(4,1)}), s8[4194304]{0:T(1024)(128)(4,1)S(1)}, s32[]{:S(2)}) async-start(s8[6291456]{0:T(1024)(128)(4,1)} %bitcast.4), calls=%async_computation | async-start | bytes 8388608
  135.8 4.5 %slice-start.1 = ((s8[6291456]{0:T(1024)(128)(4,1)}), s8[2097152]{0:T(1024)(128)(4,1)S(1)}, s32[]{:S(2)}) async-start(s8[6291456]{0:T(1024)(128)(4,1)} %bitcast.4), calls=%async_computation.1 | async-start | bytes 4194304

commit v2 on v1

--- a/solution.py
+++ b/solution.py
@@ -29,7 +29,7 @@
 def kernel(T, D, FF, NE, CAP,
            x_ref, dy_ref, rg_ref, wg_ref, wu_ref, wd_ref,
            moe_ref, gx_ref, gg_ref, dwg_ref, dwu_ref, dwd_ref,
-           xa, dya, xg, us, vs, os_, wg, wu, wd, acc, rd, fr, orv, prv,
+           xa, dya, xg, us, vs, hs, os_, wg, wu, wd, acc, rd, fr, orv, prv,
            swg, swu, swd, pb, sb, rga, rm, gm, mb, rt, gt, gga, ggs,
            ssem, rsem, lsem):
     H = T // 2
@@ -185,21 +185,17 @@
         os_[:, pl.ds(l, 1)] = o.reshape(8, 1, CAP, D)
         return carry
 
-    lax.fori_loop(0, NE, forward, 0)
-
+    lax.fori_loop(0, NE // 2, forward, 0)
     cy[1].wait_recv()
     cy[5].start()
     cy[3].wait_recv()
     cy[6].start()
-    cy[2].wait_recv()
-    cy[7].start()
-    cy[4].wait_recv()
-    cy[8].start()
+    lax.fori_loop(NE // 2, NE, forward, 0)
 
     order = (3, 1, 2, 0)
 
-    def swap_copies(b, buf):
-        return {h: rc(b + h, os_.at[2 * h + 1], buf.at[h], 1) for h in range(4)}
+    def swap_copy(b, buf, h):
+        return rc(b + h, os_.at[2 * h + 1], buf.at[h], 1)
 
     def reduce_copies(b, k):
         lo, hi = pl.ds(0, H), pl.ds(H, H)
@@ -226,21 +222,12 @@
         sb[0] = jnp.where(hit, 1.0, 0.0).astype(BF16)
         return dot(sb[0], rows)
 
-    def combine(k, h, recv, weighted):
-        a = spread(2 * h, os_[2 * h].reshape(T, D), weighted)
-        acc[k, h] = a + spread(8 + h, recv[h].reshape(T, D), weighted)
-
-    ox = swap_copies(OX, orv)
-    ro = reduce_copies(RS_O, 0)
-    for h in order:
-        ox[h].start()
-    for h in order:
-        ox[h].wait_recv()
-
-    def combine_all(k, recv, copies, weighted):
+    def combine_all(k, b, recv, copies, weighted):
         def one(i, carry):
             h = 3 - i
-            combine(k, h, recv, weighted)
+            acc[k, h] = spread(2 * h, os_[2 * h].reshape(T, D), weighted)
+            swap_copy(b, recv, h).wait_recv()
+            acc[k, h] = acc[k, h] + spread(8 + h, recv[h].reshape(T, D), weighted)
 
             @pl.when(i == 0)
             def _():
@@ -257,7 +244,14 @@
             return carry
         lax.fori_loop(0, 4, one, 0)
 
-    combine_all(0, orv, ro, True)
+    ro = reduce_copies(RS_O, 0)
+    for h in order:
+        swap_copy(OX, orv, h).start()
+    cy[2].wait_recv()
+    cy[7].start()
+    cy[4].wait_recv()
+    cy[8].start()
+    combine_all(0, OX, orv, ro, True)
 
     cy[5].wait_recv()
     cy[6].wait_recv()
@@ -290,39 +284,7 @@
     for c in ggc:
         c.start()
     for h in order:
-        ox[h].wait_send()
-
-    def finish_grads(l):
-        return [
-            pltpu.make_async_copy(swg, dwg_ref.at[l], lsem.at[5]),
-            pltpu.make_async_copy(swu, dwu_ref.at[l], lsem.at[6]),
-            pltpu.make_async_copy(swd, dwd_ref.at[l], lsem.at[7]),
-        ]
-
-    def backward(l, carry):
-        rows = xg[:, pl.ds(l, 1)].reshape(T, D)
-        c = xa[:, pl.ds(pl.multiple_of(l * CAP, CAP), CAP), :].reshape(T, D)
-        dh = dotg(c, wd[l], NT).astype(BF16).astype(F32)
-        uf = us[l].astype(F32)
-        vf = vs[l].astype(F32)
-        s = jax.nn.sigmoid(uf)
-        sl = uf * s
-        h = (sl * vf).astype(BF16)
-        dv = (dh * sl).astype(BF16)
-        du = (dh * vf * (s + sl * (1.0 - s))).astype(BF16)
-        pr = (dotg(du, wg[l], NT) + dotg(dv, wu[l], NT)).astype(BF16)
-        os_[:, pl.ds(l, 1)] = pr.reshape(8, 1, CAP, D)
-
-        @pl.when(l > 0)
-        def _():
-            for cp in finish_grads(l - 1):
-                cp.wait()
-        swd[...] = dotg(h, c, TN)
-        swg[...] = dotg(rows, du, TN)
-        swu[...] = dotg(rows, dv, TN)
-        for cp in finish_grads(l):
-            cp.start()
-        return carry
+        swap_copy(OX, orv, h).wait_send()
 
     def pass_on(k, copies):
         copies[0].wait_recv()
@@ -337,17 +299,53 @@
             copies[i].wait_recv()
         out[...] = (acc[k, 0] + fr[k, 0] + fr[k, 1]).astype(BF16)
 
-    lax.fori_loop(0, NE // 2, backward, 0)
     pass_on(0, ro)
-    lax.fori_loop(NE // 2, NE, backward, 0)
-
-    px = swap_copies(PX, prv)
+
+    def expert_rows(buf, l):
+        return buf[:, pl.ds(pl.multiple_of(l * CAP, CAP), CAP), :].reshape(T, D)
+
+    def backward(l, carry):
+        dh = dotg(expert_rows(xa, l), wd[l], NT).astype(BF16).astype(F32)
+        uf = us[l].astype(F32)
+        vf = vs[l].astype(F32)
+        s = jax.nn.sigmoid(uf)
+        sl = uf * s
+        hs[l] = (sl * vf).astype(BF16)
+        dv = (dh * sl).astype(BF16)
+        du = (dh * vf * (s + sl * (1.0 - s))).astype(BF16)
+        us[l] = du
+        vs[l] = dv
+        pr = (dotg(du, wg[l], NT) + dotg(dv, wu[l], NT)).astype(BF16)
+        os_[:, pl.ds(l, 1)] = pr.reshape(8, 1, CAP, D)
+        return carry
+
+    lax.fori_loop(0, NE, backward, 0)
+
     rp = reduce_copies(RS_P, 1)
     for h in order:
-        px[h].start()
-    for h in order:
-        px[h].wait_recv()
-    combine_all(1, prv, rp, False)
+        swap_copy(PX, prv, h).start()
+    combine_all(1, PX, prv, rp, False)
+
+    def finish_grads(l):
+        return [
+            pltpu.make_async_copy(swg, dwg_ref.at[l], lsem.at[5]),
+            pltpu.make_async_copy(swu, dwu_ref.at[l], lsem.at[6]),
+            pltpu.make_async_copy(swd, dwd_ref.at[l], lsem.at[7]),
+        ]
+
+    def weight_grads(l, carry):
+        rows = xg[:, pl.ds(l, 1)].reshape(T, D)
+
+        @pl.when(l > 0)
+        def _():
+            for cp in finish_grads(l - 1):
+                cp.wait()
+        swg[...] = dotg(rows, us[l], TN)
+        swu[...] = dotg(rows, vs[l], TN)
+        swd[...] = dotg(hs[l], expert_rows(xa, l), TN)
+        for cp in finish_grads(l):
+            cp.start()
+        return carry
 
     for c in ggc:
         c.wait_recv()
@@ -365,12 +363,17 @@
         gg_ref[j:j + 1, :] = out[j]
 
     finish(0, ro, moe_ref)
+    lax.fori_loop(0, NE // 2, weight_grads, 0)
     pass_on(1, rp)
-    finish(1, rp, gx_ref)
-
+    lax.fori_loop(NE // 2, NE, weight_grads, 0)
     for cp in finish_grads(NE - 1):
         cp.wait()
-    for c in rgc + cy + ggc + ro + rp + [px[h] for h in order]:
+    for c in rgc + cy + ggc + ro:
+        c.wait_send()
+    for h in order:
+        swap_copy(PX, prv, h).wait_send()
+    finish(1, rp, gx_ref)
+    for c in rp:
         c.wait_send()
 
 
@@ -398,6 +401,7 @@
                 pltpu.VMEM((8, T, D), BF16),
                 pltpu.VMEM((8, T, D), BF16),
                 pltpu.VMEM((8, NE, CAP, D), BF16),
+                pltpu.VMEM((NE, T, FF), BF16),
                 pltpu.VMEM((NE, T, FF), BF16),
                 pltpu.VMEM((NE, T, FF), BF16),
                 pltpu.VMEM((8, NE, CAP, D), BF16),

time: 143 us -> 136 us (0.951)
  Pallas kernels: 121 us -> 114 us
    pallas_call x1, Pallas kernels: 121 us -> 114 us  [local_step(): pl.pallas_call(functools.partial(kernel, T, D, FF, NE, CAP), out_shape=(s...]
where the time goes in v2:
time: 136 us
  Pallas kernels  114 us (84%)
  local copies, waits for them, and re-layouts  18.9 us (14%)
  other arithmetic  2.05 us (2%)
    pallas_call x1, Pallas kernels, local_step(): pl.pallas_call(functools.partial(kernel, T, D, FF, NE, CAP), out_shape=(s...  114 us
    unnamed x12, local copies, waits for them, and re-layouts  18.9 us

profile of v2, /device:TPU:0, one launch (start us, length us, event | category | flops | bytes accessed | tf_op | source)
XLA Modules:
  0.0 135.7 jit_solution(14562478422621238154)
XLA Ops:
  0.6 0.7 convert_bitcast_fusion
  1.4 1.3 pad_maximum_fusion.rg_ref
  2.7 114.1 %shard_map.118 = (bf16[512,512]{1,0:T(8,128)(2,1)}, bf16[512,512]{1,0:T(8,128)(2,1)}, f32[8,512]{1,0:T(8,128)}, f32[8,512,384]{2,1,0:T(8,128)}, f32[8,512,384]{2,1,0:T(8,128)}, /*index=5*/f32[8,384,512]{2,1,0:T(8,128)}) custom-call(bf16[512,512]{1,0:T(8,128)(2,1)} %x_ref.1, bf16[512,512]{1,0:T(8,128)(2,1)} %dy_ref.1, f32[16,512]{1,0:T(8,128)} %pad_maximum_fusion.rg_ref, ...), custom_call_target="tpu_custom_call" | custom-call | tf_op jit(solution)/shard_map/pallas_call | solution.py:394
  116.8 1.9 %copy.19 = bf16[512,512]{1,0:T(8,128)(2,1)} copy(bf16[512,512]{1,0:T(8,128)(2,1)} %get-tuple-element.24) | data formatting | bytes 1048576
  118.7 1.9 %copy.20 = bf16[512,512]{1,0:T(8,128)(2,1)} copy(bf16[512,512]{1,0:T(8,128)(2,1)} %get-tuple-element.25) | data formatting | bytes 1048576
  120.5 1.3 copy.21
  121.9 0.0 copy-start
  121.9 0.0 slice-start
  121.9 6.6 %copy.22 = f32[8,512,384]{2,1,0:T(8,128)} copy(f32[8,512,384]{2,1,0:T(8,128)} %get-tuple-element.27) | data formatting | bytes 12582912
  128.4 0.0 copy-done
  128.4 0.0 slice-start.1
  128.4 3.2 %copy.23 = f32[8,512,384]{2,1,0:T(8,128)} copy(f32[8,512,384]{2,1,0:T(8,128)S(1)} %copy-done) | data formatting | bytes 12582912
  131.6 0.0 slice-done
  131.6 1.3 slice-done.1
  133.0 2.7 %copy.24 = f32[8,384,512]{2,1,0:T(8,128)} copy(f32[8,384,512]{2,1,0:T(8,128)S(1)} %bitcast.5) | data formatting | bytes 12582912
  (1 shorter events, 0.0 us)
Async XLA Ops:
  121.9 6.6 %copy-start = (f32[8,512,384]{2,1,0:T(8,128)S(1)}, f32[8,512,384]{2,1,0:T(8,128)}, u32[]{:S(2)}) copy-start(f32[8,512,384]{2,1,0:T(8,128)} %get-tuple-element.28) | copy-start | bytes 18874372
  121.9 9.8 %slice-start = ((s8[6291456]{0:T(1024)(128)(4,1)}), s8[4194304]{0:T(1024)(128)(4,1)S(1)}, s32[]{:S(2)}) async-start(s8[6291456]{0:T(1024)(128)(4,1)} %bitcast.4), calls=%async_computation | async-start | bytes 8388608
  128.4 4.5 %slice-start.1 = ((s8[6291456]{0:T(1024)(128)(4,1)}), s8[2097152]{0:T(1024)(128)(4,1)S(1)}, s32[]{:S(2)}) async-start(s8[6291456]{0:T(1024)(128)(4,1)} %bitcast.4), calls=%async_computation.1 | async-start | bytes 4194304
